TPU v7x, 32 devices: a whole 2x2x4 slice. The times are simulated.
32 devices in a mesh: dp: 8 (over z, core), seq: 4 (over y, x).
Axes of the slice: x: 2, y: 2, z: 4, core: 2. Of those that a mesh axis runs over, the one named last changes fastest.
Arguments:
- layer_in: bfloat16 [8, 512, 2560], P('dp', 'seq'), may hold values from -6 to 6
- scan_in: bfloat16 [8, 512, 2560], P('dp', 'seq'), may hold values from -6 to 6
- step_size: float32 [8, 512, 40], P('dp', 'seq'), may hold values from 0.0024 to 0.041
- b_weight: bfloat16 [2560, 64], replicated, may hold values from -0.125 to 0.125
- c_weight: bfloat16 [2560, 64], replicated, may hold values from -0.125 to 0.125
- decay_rate: float32 [40], replicated, may hold values from 0.0005 to 10
- skip_gain: float32 [40], replicated, may hold values from 0.25 to 1.75
- out_grad: bfloat16 [8, 512, 2560], P('dp', 'seq'), may hold values from -6 to 6
- doc_lengths: int32 [8, 4], P('dp'), may hold values from 1 to 256, 512 in all within a row
- block_order: int32 [8, 4], P('dp'), may hold values from 0 to 3, each once within a row
Outputs:
- scan_out: bfloat16 [8, 512, 2560], P('dp', 'seq')
- b_weight_grad: float32 [2560, 64], replicated
- c_weight_grad: float32 [2560, 64], replicated
Inputs may be any that keep to these rules, and one draw needn't show every extreme that they name: `block_order`: each row holds 0 to 3 once each. `doc_lengths`: each row sums to 512; its longest document has 256 tokens.
All inputs are finite; a program needn't handle non-finite values.
Results may differ from a plain program's by a relative error of at most 0.0055.
Values sent between devices are 32-bit elements.
A program may use at most 128 MiB of HBM per device.

v0:
```python
import math
import jax
import jax.numpy as jnp
from jax import lax
from jax.sharding import PartitionSpec as P

precise = lax.Precision.HIGHEST


def link_weights(low_block, high_block, totals):
    block_count = totals.shape[0]
    places = jnp.arange(block_count, dtype=jnp.int32)
    inside = (low_block[:, None] < places[None, :]) & (places[None, :] < high_block[:, None])
    factors = jnp.where(inside[:, :, None], totals[None, :, :], jnp.float32(1.0))
    return jnp.prod(factors, axis=1) * (low_block < high_block).astype(jnp.float32)[:, None]


def per_device(
    layer_in,
    scan_in,
    step_size,
    b_weight,
    c_weight,
    decay_rate,
    skip_gain,
    out_grad,
    doc_lengths,
    block_order,
):
    row_count = scan_in.shape[1]
    head_count = decay_rate.shape[0]
    head_width = scan_in.shape[2] // head_count
    state_count = b_weight.shape[1]
    block_count = lax.axis_size("seq")
    group_count = lax.axis_size("dp")
    my_slot = lax.axis_index("seq")
    tokens = layer_in[0]
    b_mat = jnp.dot(tokens, b_weight, preferred_element_type=jnp.float32).astype(jnp.bfloat16)
    c_mat = jnp.dot(tokens, c_weight, preferred_element_type=jnp.float32).astype(jnp.bfloat16)
    b_float = b_mat.astype(jnp.float32)
    c_float = c_mat.astype(jnp.float32)
    order_row = block_order[0]
    my_block = lax.dynamic_index_in_dim(order_row, my_slot, 0, keepdims=False)
    lengths = doc_lengths[0]
    doc_ends = jnp.cumsum(lengths, dtype=jnp.int32)
    doc_starts = doc_ends - lengths
    positions = my_block * row_count + jnp.arange(row_count, dtype=jnp.int32)
    segment = jnp.sum((doc_starts[None, :] <= positions[:, None]).astype(jnp.int32), axis=1)
    begins = jnp.any(doc_starts[None, :] == positions[:, None], axis=1)
    step_sizes = step_size[0]
    log_rates = -step_sizes * decay_rate[None, :]
    offsets = jnp.arange(row_count, dtype=jnp.int32)
    lower_tri = offsets[:, None] >= offsets[None, :]
    cumlog = jnp.dot(lower_tri.astype(jnp.float32), log_rates, precision=precise)
    linked = (segment == segment[0]) & jnp.logical_not(begins[0])
    in_last = segment == segment[row_count - 1]
    entering = jnp.where(linked[:, None], jnp.exp(cumlog), jnp.float32(0.0))
    leaving = jnp.where(
        in_last[:, None], jnp.exp(cumlog[row_count - 1][None, :] - cumlog), jnp.float32(0.0)
    )
    block_total = entering[row_count - 1]
    x_heads = scan_in[0].reshape(row_count, head_count, head_width)
    grad_heads = out_grad[0].reshape(row_count, head_count, head_width)
    driven = x_heads.astype(jnp.float32) * step_sizes[:, :, None]
    pushed = driven * leaving[:, :, None]
    seen = grad_heads.astype(jnp.float32) * entering[:, :, None]
    own_state = jnp.einsum("thp,tn->hpn", pushed, b_float, precision=precise).reshape(
        head_count, head_width * state_count
    )
    own_adjoint = jnp.einsum("thp,tn->hpn", seen, c_float, precision=precise).reshape(
        head_count, head_width * state_count
    )
    all_totals = lax.all_gather(block_total[None, :], "seq", axis=0, tiled=True)
    held_slots = jnp.arange(block_count, dtype=jnp.int32)
    onehot = (order_row[None, :] == held_slots[:, None]).astype(jnp.float32)
    seq_totals = jnp.dot(onehot, all_totals, precision=precise)
    mine_vector = jnp.full((block_count,), my_block, jnp.int32)
    from_earlier = link_weights(order_row, mine_vector, seq_totals)
    from_later = link_weights(mine_vector, order_row, seq_totals)
    incoming = jnp.einsum(
        "ch,chz->hz",
        from_earlier,
        lax.all_gather(own_state[None], "seq", axis=0, tiled=True),
        precision=precise,
    )
    returning = jnp.einsum(
        "ch,chz->hz",
        from_later,
        lax.all_gather(own_adjoint[None], "seq", axis=0, tiled=True),
        precision=precise,
    )
    incoming = incoming.reshape(head_count, head_width, state_count)
    returning = returning.reshape(head_count, head_width, state_count)
    scores = jnp.einsum("tn,sn->ts", c_mat, b_mat, preferred_element_type=jnp.float32)
    causal = lower_tri & (segment[:, None] == segment[None, :])
    set_size = math.gcd(head_count, 16)
    set_count = head_count // set_size

    def per_set(set_index, totals_pair):
        out_acc, mix_acc = totals_pair
        head_first = set_index * set_size
        set_log = lax.dynamic_slice_in_dim(cumlog, head_first, set_size, 1)
        set_steps = lax.dynamic_slice_in_dim(step_sizes, head_first, set_size, 1)
        set_driven = lax.dynamic_slice_in_dim(driven, head_first, set_size, 1)
        set_inputs = lax.dynamic_slice_in_dim(x_heads, head_first, set_size, 1)
        set_cotan = lax.dynamic_slice_in_dim(grad_heads, head_first, set_size, 1)
        log_gaps = set_log.T[:, :, None] - set_log.T[:, None, :]
        decays = jnp.exp(jnp.where(causal[None], log_gaps, jnp.float32(-1e30)))
        mixed = decays * scores[None]
        y_part = jnp.einsum("hts,shp->thp", mixed, set_driven, precision=precise)
        intersect = jnp.einsum(
            "thp,shp->hts", set_cotan, set_inputs, preferred_element_type=jnp.float32
        )
        q_part = jnp.sum(decays * intersect * set_steps.T[:, None, :], axis=0)
        out_acc = lax.dynamic_update_slice_in_dim(out_acc, y_part, head_first, 1)
        return (out_acc, mix_acc + q_part)

    start_pair = (
        jnp.zeros((row_count, head_count, head_width), jnp.float32),
        jnp.zeros((row_count, row_count), jnp.float32),
    )
    y_intra, mixing = lax.fori_loop(0, set_count, per_set, start_pair)
    y_cross = jnp.einsum("tn,hpn->thp", c_float, incoming, precision=precise) * entering[:, :, None]
    y_total = y_intra + y_cross + skip_gain[None, :, None] * x_heads.astype(jnp.float32)
    scan_out = y_total.reshape(row_count, head_count * head_width).astype(jnp.bfloat16)[None]
    grad_c = jnp.dot(mixing, b_float, precision=precise) + jnp.einsum(
        "thp,hpn->tn", seen, incoming, precision=precise
    )
    grad_b = jnp.einsum("ts,tn->sn", mixing, c_float, precision=precise) + jnp.einsum(
        "thp,hpn->tn", pushed, returning, precision=precise
    )
    local_b = jnp.einsum(
        "td,tn->dn", tokens, grad_b.astype(jnp.bfloat16), preferred_element_type=jnp.float32
    )
    local_c = jnp.einsum(
        "td,tn->dn", tokens, grad_c.astype(jnp.bfloat16), preferred_element_type=jnp.float32
    )
    summed_b, summed_c = lax.psum((local_b, local_c), ("dp", "seq"))
    scale = 1.0 / (group_count * row_count * block_count)
    return (scan_out, summed_b * scale, summed_c * scale)


def solution(mesh):
    in_specs = (
        P("dp", "seq", None),
        P("dp", "seq", None),
        P("dp", "seq", None),
        P(),
        P(),
        P(),
        P(),
        P("dp", "seq", None),
        P("dp", None),
        P("dp", None),
    )
    out_specs = (P("dp", "seq", None), P(), P())
    return jax.shard_map(
        per_device, mesh=mesh, in_specs=in_specs, out_specs=out_specs, check_vma=False
    )
```

profile of v0, /device:TPU:0, one launch (start us, length us, event | category | flops | bytes accessed | tf_op | source)
XLA Modules:
  0.0 262.6 jit_solution(5989525888902868005)
XLA Ops:
  7.3 1.3 constant_dynamic-slice_fusion
  9.2 0.8 reduce-window_clone.1
  10.0 0.7 subtract_bitcast_fusion
  10.7 0.1 convert_reduce_fusion
  10.8 0.1 compare_reduce_fusion
  10.9 1.4 copy.37
  12.3 0.2 fusion.38
  12.6 0.2 slice_reduce_fusion
  12.7 0.6 fusion.50
  13.4 0.3 convolution_convert_fusion
  13.7 1.3 broadcast_compare_fusion
  15.1 0.8 fusion.28
  16.0 1.3 broadcast_in_dim_reshape.6
  17.3 0.3 copy.38
  17.6 0.6 copy-done.7
  18.2 0.3 convolution_convert_fusion.1
  18.5 0.8 fusion.25
  19.3 1.3 broadcast_in_dim_reshape.7
  20.7 1.3 convert_multiply_fusion.1
  22.0 0.8 fusion.51
  22.8 0.2 slice_reduce_fusion.1
  23.0 0.6 iota_compare_fusion.8
  23.6 0.6 compare_convert_fusion
  24.2 1.2 bitcast_multiply_fusion.1
  25.4 1.2 bitcast_multiply_fusion
  26.6 9.7 %all-gather = f32[4,1,40]{2,1,0:T(1,128)S(1)} all-gather(f32[1,1,40]{2,1,0:T(1,128)S(1)} %bitcast.112), channel_id=1, replica_groups=mesh['dp'=8,'seq'=4] {'seq'}, dimensions={0}, use_global_device_ids=true | all-gather | bytes 800 | tf_op jit(solution)/shard_map/all_gather | solution.py:73
  36.3 0.1 fusion.46
  36.5 0.1 select_reduce_fusion
  36.7 0.1 copy.44
  36.9 0.1 copy.47
  37.0 0.1 broadcast_in_dim.120
  37.1 13.5 %while.16 = (s32[]{:T(128)}, f32[128,40,64]{0,2,1:T(8,128)S(1)}, f32[128,128]{1,0:T(8,128)S(1)}, f32[128,40,64]{0,2,1:T(8,128)}, f32[128,40]{0,1:T(8,128)S(1)}, ...) while((s32[]{:T(128)}, f32[128,40,64]{0,2,1:T(8,128)S(1)}, ...), condition=%wide.region_4.5_spmd.clone, body=%wide.region_2.4_spmd.clone.sunk | while | flops 118554632 | bytes 1202889 | solution.py:122
  37.1 0.1 fusion.81
  37.2 2.1 fusion.82
  39.4 0.3 fusion.83
  39.8 0.1 fusion.81
  39.9 2.1 fusion.82
  42.0 0.3 fusion.83
  42.5 2.2 fusion.82
  44.7 0.3 fusion.83
  45.2 2.1 fusion.82
  47.4 0.3 fusion.83
  47.8 0.1 fusion.81
  47.9 2.1 fusion.82
  50.0 0.3 fusion.83
  50.6 9.0 %all-gather.4.cloned.1.call-done = f32[4,40,4096]{2,1,0:T(8,128)} async-done(((f32[1,40,4096]{2,1,0:T(8,128)}), f32[4,40,4096]{2,1,0:T(8,128)}) %all-gather.4.cloned.1.call-update) | async-done | bytes 2621456 | tf_op jit(solution)/shard_map/all_gather | solution.py:83
  59.7 8.0 %fusion.20 = f32[40,1,4096]{2,1,0:T(1,128)S(1)} fusion(f32[4,40,1]{0,2,1:T(1,128)S(1)} %copy.44, f32[4,40,4096]{2,1,0:T(8,128)} %all-gather.4.cloned.1.call-done), kind=kOutput, calls=%fused_computation.28 | convolution fusion | flops 7864320 | bytes 3277440 | tf_op jit(solution)/shard_map/ch,chz->hz/dot_general | solution.py:80
  67.6 1.2 copy.59
  68.9 1.7 reshape.147
  70.5 31.1 %all-gather.6.cloned.1.call-done = f32[4,40,4096]{2,1,0:T(8,128)} async-done(((f32[1,40,4096]{2,1,0:T(8,128)}), f32[4,40,4096]{2,1,0:T(8,128)}) %all-gather.6.cloned.1.call-update) | async-done | bytes 2621456 | tf_op jit(solution)/shard_map/all_gather | solution.py:89
  101.6 8.2 %fusion.18 = f32[40,1,4096]{2,1,0:T(1,128)S(1)} fusion(f32[4,40,1]{0,2,1:T(1,128)S(1)} %copy.47, f32[4,40,4096]{2,1,0:T(8,128)} %all-gather.6.cloned.1.call-done), kind=kOutput, calls=%fused_computation.26 | convolution fusion | flops 7864320 | bytes 3277440 | tf_op jit(solution)/shard_map/ch,chz->hz/dot_general | solution.py:86
  109.8 0.4 copy.58
  110.2 1.6 reshape.148
  111.8 4.0 %convolution_bitcast_fusion.4 = f32[128,64]{0,1:T(8,128)S(1)} fusion(f32[128,40,64]{0,2,1:T(8,128)} %bitcast.101, f32[40,64,64]{2,1,0:T(8,128)} %reshape.148), kind=kOutput, calls=%fused_computation.47 | convolution fusion | flops 251658240 | bytes 1998848 | tf_op jit(solution)/shard_map/thp,hpn->tn/dot_general | solution.py:129
  115.8 0.2 fusion.30
  116.0 1.1 convolution_bitcast_fusion.2
  117.1 2.3 convolution_bitcast_fusion.3
  119.5 0.2 fusion.31
  119.7 1.1 convolution_bitcast_fusion.1
  120.8 2.2 fusion.24
  123.0 1.1 copy.43
  124.1 129.1 %all-reduce.3.cloned.1.call-done = (f32[2560,64]{0,1:T(8,128)}, f32[2560,64]{0,1:T(8,128)}) async-done(((f32[2560,64]{0,1:T(8,128)}, f32[2560,64]{0,1:T(8,128)}), (f32[2560,64]{0,1:T(8,128)}, f32[2560,64]{0,1:T(8,128)})) %all-reduce.3.cloned.1.call-update) | async-done | bytes 1310736 | tf_op jit(solution)/shard_map/psum | solution.py:138
  253.1 2.0 broadcast_multiply_fusion.1
  255.2 0.9 broadcast_multiply_fusion
  (45 shorter events, 0.9 us)
Async XLA Ops:
  7.2 6.2 %copy-start = (bf16[1,128,2560]{2,1,0:T(8,128)(2,1)S(1)}, bf16[1,128,2560]{2,1,0:T(8,128)(2,1)}, u32[]{:S(2)}) copy-start(bf16[1,128,2560]{2,1,0:T(8,128)(2,1)} %param.12) | copy-start | bytes 1966084
  7.2 5.1 %copy-start.5 = (f32[1,128,40]{1,2,0:T(8,128)S(1)}, f32[1,128,40]{1,2,0:T(8,128)}, u32[]{:S(2)}) copy-start(f32[1,128,40]{1,2,0:T(8,128)} %param.14) | copy-start | bytes 61444
  7.2 5.1 %copy-start.10 = (f32[40]{0:T(128)S(1)}, f32[40]{0:T(128)}, u32[]{:S(2)}) copy-start(f32[40]{0:T(128)} %param.17) | copy-start | bytes 484
  7.2 6.2 %copy-start.6 = (bf16[2560,64]{0,1:T(8,128)(2,1)S(1)}, bf16[2560,64]{0,1:T(8,128)(2,1)}, u32[]{:S(2)}) copy-start(bf16[2560,64]{0,1:T(8,128)(2,1)} %param.15) | copy-start | bytes 983044
  7.2 52.4 %all-gather.4.cloned.1.call-start = ((), (), s32[]{:S(2)}) async-start(), calls=%async_computation | async-start | bytes 3276800 | tf_op jit(solution)/shard_map/all_gather | solution.py:83
  15.9 1.4 copy-start.3
  17.2 1.0 copy-start.7
  17.3 84.4 %all-gather.6.cloned.1.call-start = ((), (), s32[]{:S(2)}) async-start(), calls=%async_computation.1 | async-start | bytes 3276800 | tf_op jit(solution)/shard_map/all_gather | solution.py:89
  20.6 3.0 %copy-start.8 = (s32[1,4]{1,0:T(1,128)S(1)}, s32[1,4]{1,0:T(1,128)}, u32[]{:S(2)}) copy-start(s32[1,4]{1,0:T(1,128)} %param.21) | copy-start | bytes 52
  20.6 232.5 %all-reduce.3.cloned.1.call-start = ((), (), s32[]{:S(2)}) async-start(), calls=%async_computation.2 | async-start | bytes 2621440 | tf_op jit(solution)/shard_map/psum | solution.py:138
  50.6 17.0 %copy-start.1 = (f32[128,40,64]{0,2,1:T(8,128)}, f32[128,40,64]{0,2,1:T(8,128)S(1)}, u32[]{:S(2)}) copy-start(f32[128,40,64]{0,2,1:T(8,128)S(1)} %get-tuple-element.173) | copy-start | bytes 3932164
  115.8 1.3 copy-start.2
  119.7 1.1 copy-start.9
  253.1 2.0 copy-start.4
Sparse Core Ops, SparseCore 0:
  17.4 42.2 all-gather.3
  62.1 39.5 all-gather.5
  120.9 132.1 all-reduce.2
where the time goes:
time: 263 us
  waiting for transfers between devices  169 us (64%)
  matrix products  43.1 us (16%)
  between operations  14.7 us (6%)
  local copies, waits for them, and re-layouts  13.5 us (5%)
  other arithmetic  11.7 us (4%)
  blocking collectives  9.7 us (4%)
    psum x1, waiting for transfers between devices, per_device(): summed_b, summed_c = lax.psum((local_b, local_c), ('dp', 'seq'))  129 us
    all_gather x1, waiting for transfers between devices, per_device(): lax.all_gather(own_adjoint[None], 'seq', axis=0, tiled=True)  31.1 us
    dot_general x5, matrix products, per_set(): y_part = jnp.einsum('hts,shp->thp', mixed, set_driven, precision=precise)  10.7 us
    all_gather x1, blocking collectives, per_device(): all_totals = lax.all_gather(block_total[None, :], 'seq', axis=0, tiled=True)  9.7 us
    all_gather x1, waiting for transfers between devices, per_device(): lax.all_gather(own_state[None], 'seq', axis=0, tiled=True)  9.04 us
    dot_general x1, matrix products, per_device(): jnp.einsum('ch,chz->hz', from_later, lax.all_gather(own_adjoint[None], 's...  8.21 us
    dot_general x1, matrix products, per_device(): jnp.einsum('ch,chz->hz', from_earlier, lax.all_gather(own_state[None], 's...  7.98 us
  transfers between devices with their start and end apart: 3, of which 3 were waited for; matrix products, arithmetic and copies ran while one was open for 14% of the time, Pallas kernels for 0%

commit v1 on v0

--- a/solution.py
+++ b/solution.py
@@ -135,7 +135,7 @@
     local_c = jnp.einsum(
         "td,tn->dn", tokens, grad_c.astype(jnp.bfloat16), preferred_element_type=jnp.float32
     )
-    summed_b, summed_c = lax.psum((local_b, local_c), ("dp", "seq"))
+    summed_b, summed_c = lax.psum(lax.psum((local_b, local_c), "seq"), "dp")
     scale = 1.0 / (group_count * row_count * block_count)
     return (scan_out, summed_b * scale, summed_c * scale)
 

time: 263 us -> 252 us (0.958)
  waiting for transfers between devices: 169 us -> 156 us
    psum x1 -> x2, waiting for transfers between devices: 129 us -> 116 us  [per_device(): summed_b, summed_c = lax.psum(lax.psum((local_b, local_c), 'seq'), 'dp')]
  transfers between devices with their start and end apart: 3 -> 4, of which waited for: 3 -> 4; matrix products, arithmetic and copies ran while one was open for 14% -> 15% of each run, Pallas kernels for 0% -> 0%
where the time goes in v1:
time: 252 us
  waiting for transfers between devices  156 us (62%)
  matrix products  43.1 us (17%)
  local copies, waits for them, and re-layouts  16 us (6%)
  between operations  14.7 us (6%)
  other arithmetic  11.8 us (5%)
  blocking collectives  9.69 us (4%)
    psum x2, waiting for transfers between devices, per_device(): summed_b, summed_c = lax.psum(lax.psum((local_b, local_c), 'seq'), 'dp')  116 us
    all_gather x1, waiting for transfers between devices, per_device(): lax.all_gather(own_adjoint[None], 'seq', axis=0, tiled=True)  31.1 us
    dot_general x5, matrix products, per_set(): y_part = jnp.einsum('hts,shp->thp', mixed, set_driven, precision=precise)  10.7 us
    all_gather x1, blocking collectives, per_device(): all_totals = lax.all_gather(block_total[None, :], 'seq', axis=0, tiled=True)  9.69 us
    all_gather x1, waiting for transfers between devices, per_device(): lax.all_gather(own_state[None], 'seq', axis=0, tiled=True)  8.45 us
    dot_general x1, matrix products, per_device(): jnp.einsum('ch,chz->hz', from_later, lax.all_gather(own_adjoint[None], 's...  8.21 us
    dot_general x1, matrix products, per_device(): jnp.einsum('ch,chz->hz', from_earlier, lax.all_gather(own_state[None], 's...  7.98 us
  transfers between devices with their start and end apart: 4, of which 4 were waited for; matrix products, arithmetic and copies ran while one was open for 15% of the time, Pallas kernels for 0%

profile of v1, /device:TPU:0, one launch (start us, length us, event | category | flops | bytes accessed | tf_op | source)
XLA Modules:
  0.0 251.6 jit_solution(13996045241390826835)
XLA Ops:
  7.3 1.3 constant_dynamic-slice_fusion
  9.2 0.8 reduce-window_clone.1
  10.0 0.7 subtract_bitcast_fusion
  10.7 0.1 convert_reduce_fusion
  10.8 0.1 compare_reduce_fusion
  10.9 1.4 copy.37
  12.3 0.2 fusion.38
  12.6 0.2 slice_reduce_fusion
  12.7 0.6 fusion.50
  13.4 0.3 convolution_convert_fusion
  13.7 1.3 broadcast_compare_fusion
  15.1 0.8 fusion.28
  15.9 1.3 broadcast_in_dim_reshape.6
  17.3 1.4 copy.38
  18.8 0.3 convolution_convert_fusion.1
  19.1 0.8 fusion.25
  19.9 1.3 broadcast_in_dim_reshape.7
  21.2 1.3 convert_multiply_fusion.1
  22.6 0.8 fusion.51
  23.4 0.2 slice_reduce_fusion.1
  23.6 0.6 iota_compare_fusion.8
  24.2 0.6 compare_convert_fusion
  24.8 1.2 bitcast_multiply_fusion.1
  26.0 1.2 bitcast_multiply_fusion
  27.2 9.7 %all-gather = f32[4,1,40]{2,1,0:T(1,128)S(1)} all-gather(f32[1,1,40]{2,1,0:T(1,128)S(1)} %bitcast.112), channel_id=1, replica_groups=mesh['dp'=8,'seq'=4] {'seq'}, dimensions={0}, use_global_device_ids=true | all-gather | bytes 800 | tf_op jit(solution)/shard_map/all_gather | solution.py:73
  36.9 0.1 fusion.46
  37.1 0.1 select_reduce_fusion
  37.3 0.1 copy.44
  37.4 0.1 copy.47
  37.5 0.1 broadcast_in_dim.120
  37.7 13.5 %while.16 = (s32[]{:T(128)}, f32[128,40,64]{0,2,1:T(8,128)S(1)}, f32[128,128]{1,0:T(8,128)S(1)}, f32[128,40,64]{0,2,1:T(8,128)}, f32[128,40]{0,1:T(8,128)S(1)}, ...) while((s32[]{:T(128)}, f32[128,40,64]{0,2,1:T(8,128)S(1)}, ...), condition=%wide.region_4.5_spmd.clone, body=%wide.region_2.4_spmd.clone.sunk | while | flops 118554632 | bytes 1202889 | solution.py:122
  37.8 2.1 fusion.82
  40.0 0.3 fusion.83
  40.4 0.1 fusion.81
  40.5 2.1 fusion.82
  42.6 0.3 fusion.83
  43.0 0.1 fusion.81
  43.1 2.2 fusion.82
  45.3 0.3 fusion.83
  45.7 0.1 fusion.81
  45.8 2.1 fusion.82
  48.0 0.3 fusion.83
  48.5 2.1 fusion.82
  50.6 0.3 fusion.83
  51.2 8.4 %all-gather.4.cloned.1.call-done = f32[4,40,4096]{2,1,0:T(8,128)} async-done(((f32[1,40,4096]{2,1,0:T(8,128)}), f32[4,40,4096]{2,1,0:T(8,128)}) %all-gather.4.cloned.1.call-update) | async-done | bytes 2621456 | tf_op jit(solution)/shard_map/all_gather | solution.py:83
  59.6 8.0 %fusion.20 = f32[40,1,4096]{2,1,0:T(1,128)S(1)} fusion(f32[4,40,1]{0,2,1:T(1,128)S(1)} %copy.44, f32[4,40,4096]{2,1,0:T(8,128)} %all-gather.4.cloned.1.call-done), kind=kOutput, calls=%fused_computation.28 | convolution fusion | flops 7864320 | bytes 3277440 | tf_op jit(solution)/shard_map/ch,chz->hz/dot_general | solution.py:80
  67.6 1.2 copy.59
  68.8 1.7 reshape.147
  70.5 31.1 %all-gather.6.cloned.1.call-done = f32[4,40,4096]{2,1,0:T(8,128)} async-done(((f32[1,40,4096]{2,1,0:T(8,128)}), f32[4,40,4096]{2,1,0:T(8,128)}) %all-gather.6.cloned.1.call-update) | async-done | bytes 2621456 | tf_op jit(solution)/shard_map/all_gather | solution.py:89
  101.6 8.2 %fusion.18 = f32[40,1,4096]{2,1,0:T(1,128)S(1)} fusion(f32[4,40,1]{0,2,1:T(1,128)S(1)} %copy.47, f32[4,40,4096]{2,1,0:T(8,128)} %all-gather.6.cloned.1.call-done), kind=kOutput, calls=%fused_computation.26 | convolution fusion | flops 7864320 | bytes 3277440 | tf_op jit(solution)/shard_map/ch,chz->hz/dot_general | solution.py:86
  109.8 1.2 copy.58
  111.0 2.7 %reshape.148 = f32[40,64,64]{2,1,0:T(8,128)} reshape(f32[40,4096]{1,0:T(8,128)} %bitcast.104) | data formatting | bytes 1310720 | tf_op jit(solution)/shard_map/reshape | solution.py:93
  113.7 4.0 %convolution_bitcast_fusion.4 = f32[128,64]{0,1:T(8,128)S(1)} fusion(f32[128,40,64]{0,2,1:T(8,128)} %bitcast.101, f32[40,64,64]{2,1,0:T(8,128)} %reshape.148), kind=kOutput, calls=%fused_computation.47 | convolution fusion | flops 251658240 | bytes 1998848 | tf_op jit(solution)/shard_map/thp,hpn->tn/dot_general | solution.py:129
  117.7 0.2 fusion.30
  117.9 1.1 convolution_bitcast_fusion.2
  119.1 2.3 convolution_bitcast_fusion.3
  121.4 0.2 fusion.31
  121.6 1.1 convolution_bitcast_fusion.1
  122.7 56.5 %all-reduce.7.cloned.1.call-done = (f32[2560,64]{0,1:T(8,128)}, f32[2560,64]{0,1:T(8,128)}) async-done(((f32[2560,64]{0,1:T(8,128)}, f32[2560,64]{0,1:T(8,128)}), (f32[2560,64]{0,1:T(8,128)}, f32[2560,64]{0,1:T(8,128)})) %all-reduce.7.cloned.1.call-update) | async-done | bytes 1310736 | tf_op jit(solution)/shard_map/psum | solution.py:138
  179.3 2.2 fusion.24
  181.4 1.1 copy.43
  182.5 59.6 %all-reduce.5.cloned.1.call-done = (f32[2560,64]{0,1:T(8,128)}, f32[2560,64]{0,1:T(8,128)}) async-done(((f32[2560,64]{0,1:T(8,128)}, f32[2560,64]{0,1:T(8,128)}), (f32[2560,64]{0,1:T(8,128)}, f32[2560,64]{0,1:T(8,128)})) %all-reduce.5.cloned.1.call-update) | async-done | bytes 1310736 | tf_op jit(solution)/shard_map/psum | solution.py:138
  242.1 2.0 broadcast_multiply_fusion.1
  244.2 0.9 broadcast_multiply_fusion
  (46 shorter events, 0.9 us)
Async XLA Ops:
  7.2 6.2 %copy-start = (bf16[1,128,2560]{2,1,0:T(8,128)(2,1)S(1)}, bf16[1,128,2560]{2,1,0:T(8,128)(2,1)}, u32[]{:S(2)}) copy-start(bf16[1,128,2560]{2,1,0:T(8,128)(2,1)} %param.12) | copy-start | bytes 1966084
  7.2 5.1 %copy-start.4 = (f32[1,128,40]{1,2,0:T(8,128)S(1)}, f32[1,128,40]{1,2,0:T(8,128)}, u32[]{:S(2)}) copy-start(f32[1,128,40]{1,2,0:T(8,128)} %param.14) | copy-start | bytes 61444
  7.2 5.1 %copy-start.9 = (f32[40]{0:T(128)S(1)}, f32[40]{0:T(128)}, u32[]{:S(2)}) copy-start(f32[40]{0:T(128)} %param.17) | copy-start | bytes 484
  7.2 6.2 %copy-start.5 = (bf16[2560,64]{0,1:T(8,128)(2,1)S(1)}, bf16[2560,64]{0,1:T(8,128)(2,1)}, u32[]{:S(2)}) copy-start(bf16[2560,64]{0,1:T(8,128)(2,1)} %param.15) | copy-start | bytes 983044
  7.2 52.4 %all-gather.4.cloned.1.call-start = ((), (), s32[]{:S(2)}) async-start(), calls=%async_computation | async-start | bytes 3276800 | tf_op jit(solution)/shard_map/all_gather | solution.py:83
  17.2 1.5 copy-start.6
  17.2 84.4 %all-gather.6.cloned.1.call-start = ((), (), s32[]{:S(2)}) async-start(), calls=%async_computation.1 | async-start | bytes 3276800 | tf_op jit(solution)/shard_map/all_gather | solution.py:89
  21.1 3.1 %copy-start.7 = (s32[1,4]{1,0:T(1,128)S(1)}, s32[1,4]{1,0:T(1,128)}, u32[]{:S(2)}) copy-start(s32[1,4]{1,0:T(1,128)} %param.21) | copy-start | bytes 52
  21.2 158.0 %all-reduce.7.cloned.1.call-start = ((), (), s32[]{:S(2)}) async-start(), calls=%async_computation.3 | async-start | bytes 2621440 | tf_op jit(solution)/shard_map/psum | solution.py:138
  51.2 16.4 %copy-start.1 = (f32[128,40,64]{0,2,1:T(8,128)}, f32[128,40,64]{0,2,1:T(8,128)S(1)}, u32[]{:S(2)}) copy-start(f32[128,40,64]{0,2,1:T(8,128)S(1)} %get-tuple-element.173) | copy-start | bytes 3932164
  117.7 1.3 copy-start.2
  122.7 56.6 %copy-start.8 = (f32[40]{0:T(128)S(1)}, f32[40]{0:T(128)}, u32[]{:S(2)}) copy-start(f32[40]{0:T(128)} %param.18) | copy-start | bytes 484
  122.7 119.5 %all-reduce.5.cloned.1.call-start = ((), (), s32[]{:S(2)}) async-start(), calls=%async_computation.2 | async-start | bytes 2621440 | tf_op jit(solution)/shard_map/psum | solution.py:138
  242.1 2.0 copy-start.3
Sparse Core Ops, SparseCore 0:
  17.4 42.2 all-gather.3
  62.1 39.4 all-gather.5
  122.8 56.3 all-reduce.6
  181.5 60.6 all-reduce.4
